TPU v7x, 32 devices: a whole 2x2x4 slice. The times are simulated.
32 devices in a mesh: node: 8 (over y, x, core), grp: 4 (over z).
Axes of the slice: x: 2, y: 2, z: 4, core: 2. Of those that a mesh axis runs over, the one named last changes fastest.
Arguments:
- tokens: bfloat16 [12288, 1792], P(('node', 'grp')), may hold values from -6 to 6
- cotangent: bfloat16 [12288, 1792], P(('node', 'grp')), may hold values from -6 to 6
- gate_weight: bfloat16 [1792, 1024], P('node'), may hold values from -0.125 to 0.125
- up_weight: bfloat16 [1792, 1024], P('node'), may hold values from -0.125 to 0.125
- down_weight_t: bfloat16 [1792, 1024], P('node'), may hold values from -0.125 to 0.125
- error_memory: bfloat16 [4, 1792, 3072], P('grp', 'node'), may hold values from -4 to 4
- q_init: float32 [3, 1024, 32], replicated, may hold values from -6 to 6
Outputs:
- token_grad: bfloat16 [12288, 1792], P(('node', 'grp'))
- new_error: bfloat16 [4, 1792, 3072], P('grp', 'node')
- p_hat: float32 [3, 1792, 32], P(None, 'node')
- q_new: float32 [3, 1024, 32], replicated
All inputs are finite; a program needn't handle non-finite values.
Results may differ from a plain program's by a relative error of at most 0.012.
Values may be sent and summed in bfloat16 or wider, within the bound.
A program may use at most 192 MiB of HBM per device.

v0:
```python
import math
import jax
import jax.numpy as jnp
from jax import lax
from jax.sharding import PartitionSpec as P


def gelu_parts(value):
    coeff = math.sqrt(2.0 / math.pi)
    inner = coeff * (value + 0.044715 * value * value * value)
    tanh_value = jnp.tanh(inner)
    activation = 0.5 * value * (1.0 + tanh_value)
    slope = 0.5 * (1.0 + tanh_value) + 0.5 * value * (1.0 - tanh_value * tanh_value) * coeff * (
        1.0 + 3.0 * 0.044715 * value * value
    )
    return (activation, slope)


def contract_rows(left_side, right_side):
    return lax.dot_general(
        left_side, right_side, (((0,), (0,)), ((), ())), preferred_element_type=jnp.float32
    )


def on_device(tokens, cotangent, gate_weight, up_weight, down_weight_t, error_memory, q_init):
    node_count = lax.axis_size("node")
    group_count = lax.axis_size("grp")
    hidden_units = gate_weight.shape[1]
    highest = lax.Precision.HIGHEST
    full_gate, full_up, full_down = (
        lax.all_gather(gate_weight, "node", axis=0, tiled=True),
        lax.all_gather(up_weight, "node", axis=0, tiled=True),
        lax.all_gather(down_weight_t, "node", axis=0, tiled=True),
    )
    gate_pre = jnp.dot(tokens, full_gate, preferred_element_type=jnp.float32)
    up_pre = jnp.dot(tokens, full_up, preferred_element_type=jnp.float32)
    activation, slope = gelu_parts(gate_pre)
    hidden = (activation * up_pre).astype(jnp.bfloat16)
    back_hidden = jnp.dot(cotangent, full_down, preferred_element_type=jnp.float32)
    grad_up = (back_hidden * activation).astype(jnp.bfloat16)
    grad_gate = (back_hidden * up_pre * slope).astype(jnp.bfloat16)
    token_grad = (
        lax.dot_general(
            grad_gate, full_gate, (((1,), (1,)), ((), ())), preferred_element_type=jnp.float32
        )
        + lax.dot_general(
            grad_up, full_up, (((1,), (1,)), ((), ())), preferred_element_type=jnp.float32
        )
    ).astype(jnp.bfloat16)
    gate_up = jnp.concatenate([grad_gate, grad_up], axis=1)
    token_cols, cot_cols = (
        lax.all_to_all(tokens, "node", split_axis=1, concat_axis=0, tiled=True),
        lax.all_to_all(cotangent, "node", split_axis=1, concat_axis=0, tiled=True),
    )
    piece_gu = lax.all_gather(gate_up, "node", axis=0, tiled=True)
    piece_hidden = lax.all_gather(hidden, "node", axis=0, tiled=True)
    summed = jnp.concatenate(
        [contract_rows(token_cols, piece_gu), contract_rows(cot_cols, piece_hidden)], axis=1
    )
    grad_scale = 1.0 / math.sqrt(tokens.shape[0] * node_count)
    merged = summed * grad_scale + error_memory[0].astype(jnp.float32)
    blocks = [merged[:, m * hidden_units : (m + 1) * hidden_units] for m in range(3)]
    row_terms = jnp.stack([jnp.dot(blocks[m], q_init[m], precision=highest) for m in range(3)])
    power_rows = lax.psum(row_terms.astype(jnp.bfloat16), "grp").astype(jnp.float32) / group_count
    local_gram = jnp.einsum("mdr,mds->mrs", power_rows, power_rows, precision=highest)
    gram_matrix = lax.psum(local_gram, "node")
    hats = []
    for m in range(3):
        factor = jnp.linalg.cholesky(gram_matrix[m])
        hats.append(jax.scipy.linalg.solve_triangular(factor, power_rows[m].T, lower=True).T)
    col_terms = jnp.stack([jnp.dot(blocks[m].T, hats[m], precision=highest) for m in range(3)])
    q_new = lax.psum(col_terms, ("node", "grp")) / group_count
    errors = [blocks[m] - jnp.dot(hats[m], q_new[m].T, precision=highest) for m in range(3)]
    new_error = jnp.concatenate(errors, axis=1).astype(jnp.bfloat16)[None]
    return (token_grad, new_error, jnp.stack(hats), q_new)


def solution(mesh):
    return jax.shard_map(
        on_device,
        mesh=mesh,
        in_specs=(
            P(("node", "grp"), None),
            P(("node", "grp"), None),
            P("node", None),
            P("node", None),
            P("node", None),
            P("grp", "node", None),
            P(),
        ),
        out_specs=(P(("node", "grp"), None), P("grp", "node", None), P(None, "node", None), P()),
        check_vma=False,
    )
```

profile of v0, /device:TPU:0, one launch (start us, length us, event | category | flops | bytes accessed | tf_op | source)
XLA Modules:
  0.0 512.1 jit_solution(15546751805123783097)
XLA Ops:
  9.4 37.6 %all-gather.6.cloned.1.call-done = bf16[1792,1024]{1,0:T(8,128)(2,1)} async-done(((bf16[224,1024]{1,0:T(8,128)(2,1)}), bf16[1792,1024]{1,0:T(8,128)(2,1)}) %all-gather.6.cloned.1.call-update) | async-done | bytes 3670032 | tf_op jit(solution)/shard_map/all_gather | solution.py:33
  47.0 5.2 %fusion.44 = f32[384,1024]{1,0:T(8,128)} fusion(bf16[384,1792]{1,0:T(8,128)(2,1)} %param.11, bf16[1792,1024]{1,0:T(8,128)(2,1)} %all-gather.6.cloned.1.call-done), kind=kOutput, calls=%fused_computation.92 | convolution fusion | flops 1409286144 | bytes 6619136 | tf_op jit(solution)/shard_map/dot_general | solution.py:39
  52.2 31.1 %all-gather.10.cloned.1.call-done = bf16[1792,1024]{1,0:T(8,128)(2,1)} async-done(((bf16[224,1024]{1,0:T(8,128)(2,1)}), bf16[1792,1024]{1,0:T(8,128)(2,1)}) %all-gather.10.cloned.1.call-update) | async-done | bytes 3670032 | tf_op jit(solution)/shard_map/all_gather | solution.py:31
  83.3 4.8 fusion.45
  88.1 31.5 %all-gather.8.cloned.1.call-done = bf16[1792,1024]{1,0:T(8,128)(2,1)} async-done(((bf16[224,1024]{1,0:T(8,128)(2,1)}), bf16[1792,1024]{1,0:T(8,128)(2,1)}) %all-gather.8.cloned.1.call-update) | async-done | bytes 3670032 | tf_op jit(solution)/shard_map/all_gather | solution.py:32
  119.6 6.4 %multiply_convert_fusion = (bf16[384,1024]{1,0:T(8,128)(2,1)}, bf16[384,1024]{1,0:T(8,128)(2,1)S(1)}, bf16[384,1024]{1,0:T(8,128)(2,1)S(1)}) fusion(f32[384,1024]{1,0:T(8,128)} %fusion.45, f32[384,1024]{1,0:T(8,128)} %fusion.44, bf16[384,1792]{1,0:T(8,128)(2,1)S(1)} %copy-done.2, bf16[1792,1024]{1,0:T(8,128)(2,1)} %all-gather.8.cloned.1.call-done), kind=kOutput, calls=%fused_computation.15 | convolution fusion | flops 1419116544 | bytes 10551296 | tf_op jit(solution)/shard_map/dot_general | solution.py:36
  126.9 1.4 pad_maximum_fusion
  128.3 1.3 copy-done.1
  129.6 1.5 copy.17
  131.1 3.6 all-to-all-start.1
  134.7 1.5 copy.15
  136.3 24.3 %all-to-all-done.1 = bf16[384,8,224]{0,2,1:T(8,128)(2,1)S(1)} async-done(((bf16[384,8,224]{0,2,1:T(8,128)(2,1)}), bf16[384,8,224]{0,2,1:T(8,128)(2,1)S(1)}, u32[]{:S(2)}, u32[]{:S(2)}) %all-to-all-start.1) | async-done | bytes 1376288 | tf_op jit(solution)/shard_map/all_to_all | solution.py:53
  160.5 3.6 all-to-all-start
  164.3 1.3 copy.25
  165.7 31.9 %all-to-all-done = bf16[384,8,224]{0,2,1:T(8,128)(2,1)S(1)} async-done(((bf16[384,8,224]{0,2,1:T(8,128)(2,1)}), bf16[384,8,224]{0,2,1:T(8,128)(2,1)S(1)}, u32[]{:S(2)}, u32[]{:S(2)}) %all-to-all-start) | async-done | bytes 1376288 | tf_op jit(solution)/shard_map/all_to_all | solution.py:52
  197.6 1.3 copy.24
  198.9 5.4 %fusion.46 = f32[384,1792]{1,0:T(8,128)} fusion(bf16[384,1024]{1,0:T(8,128)(2,1)S(1)} %copy-done.8, bf16[1792,1024]{1,0:T(8,128)(2,1)} %all-gather.10.cloned.1.call-done), kind=kOutput, calls=%fused_computation.94 | convolution fusion | flops 1409286144 | bytes 7208960 | tf_op jit(solution)/shard_map/dot_general | solution.py:43
  204.3 5.4 %convolution_bitcast_fusion.1 = f32[224,1024]{1,0:T(8,128)} fusion(bf16[3072,224]{0,1:T(8,128)(2,1)S(1)} %bitcast.133, bf16[3072,1024]{1,0:T(8,128)(2,1)} %all-gather.14.cloned.1.call-done), kind=kOutput, calls=%fused_computation.19 | convolution fusion | flops 1409286144 | bytes 8585216 | tf_op jit(solution)/shard_map/dot_general | solution.py:20
  209.7 64.7 %all-gather.12.cloned.1.call-done = bf16[3072,2048]{1,0:T(8,128)(2,1)} async-done(((bf16[384,2048]{1,0:T(8,128)(2,1)}), bf16[3072,2048]{1,0:T(8,128)(2,1)}) %all-gather.12.cloned.1.call-update) | async-done | bytes 12582928 | tf_op jit(solution)/shard_map/all_gather | solution.py:55
  274.4 6.4 %convolution_bitcast_fusion = f32[224,2048]{1,0:T(8,128)S(1)} fusion(bf16[3072,224]{0,1:T(8,128)(2,1)S(1)} %bitcast.134, bf16[3072,2048]{1,0:T(8,128)(2,1)} %all-gather.12.cloned.1.call-done), kind=kOutput, calls=%fused_computation.4 | convolution fusion | flops 2818572288 | bytes 15794176 | tf_op jit(solution)/shard_map/dot_general | solution.py:20
  285.2 20.5 %psum.21 = bf16[3,224,32]{1,2,0:T(8,128)(2,1)} all-reduce(bf16[3,224,32]{1,2,0:T(8,128)(2,1)} %pad_maximum_fusion.4), channel_id=1, replica_groups=mesh['node'=8,'grp'=4] {'grp'}, use_global_device_ids=true, to_apply=%region_0.0 | all-reduce | flops 21504 | bytes 86016 | tf_op jit(solution)/shard_map/psum | solution.py:64
  305.6 1.7 fusion.33
  307.4 1.4 convert_multiply_fusion
  308.8 24.0 %psum.22 = f32[3,32,32]{1,2,0:T(8,128)} all-reduce(f32[3,32,32]{1,2,0:T(8,128)} %fusion.33), channel_id=1, replica_groups=mesh['node'=8,'grp'=4] {'node'}, use_global_device_ids=true, to_apply=%region_1.0 | all-reduce | flops 3072 | bytes 24576 | tf_op jit(solution)/shard_map/psum | solution.py:66
  332.9 1.4 slice_bitcast_fusion.14
  335.0 1.4 copy.22
  336.4 1.4 copy.21
  337.8 1.4 fusion.39
  339.2 3.6 cholesky.59
  343.5 1.3 fusion.34
  344.8 3.8 custom-call.7
  348.5 3.6 cholesky.70
  352.9 1.3 fusion.35
  354.1 3.2 custom-call.8
  357.3 1.6 fusion.32
  358.9 1.6 fusion.31
  360.5 3.6 cholesky.81
  364.8 1.3 fusion.36
  366.0 3.2 custom-call.9
  369.2 1.0 fusion.30
  370.9 1.4 convolution_bitcast_fusion.3
  373.8 5.7 %fusion = bf16[384,1792]{1,0:T(8,128)(2,1)} fusion(f32[384,1792]{1,0:T(8,128)} %fusion.46, bf16[384,1024]{1,0:T(8,128)(2,1)S(1)} %get-tuple-element.8, bf16[1792,1024]{1,0:T(8,128)(2,1)} %all-gather.8.cloned.1.call-done), kind=kOutput, calls=%fused_computation.1 | convolution fusion | flops 1410662400 | bytes 8585216 | tf_op jit(solution)/shard_map/dot_general | solution.py:46
  380.2 119.2 %all-reduce.2.cloned.1.call-done = f32[3,1024,32]{1,2,0:T(8,128)} async-done(((f32[3,1024,32]{1,2,0:T(8,128)}), f32[3,1024,32]{1,2,0:T(8,128)}) %all-reduce.2.cloned.1.call-update) | async-done | bytes 393232 | tf_op jit(solution)/shard_map/psum | solution.py:72
  499.4 1.0 broadcast_multiply_fusion
  500.4 1.8 fusion.12
  502.2 0.9 fusion.13
  503.1 0.9 fusion.14
  504.1 1.2 pad_maximum_fusion.1
  (62 shorter events, 13.3 us)
Async XLA Ops:
  7.2 39.8 %all-gather.6.cloned.1.call-start = ((), (), s32[]{:S(2)}) async-start(), calls=%async_computation.2 | async-start | bytes 4128768 | tf_op jit(solution)/shard_map/all_gather | solution.py:33
  7.9 75.4 %all-gather.10.cloned.1.call-start = ((), (), s32[]{:S(2)}) async-start(), calls=%async_computation.4 | async-start | bytes 4128768 | tf_op jit(solution)/shard_map/all_gather | solution.py:31
  8.6 111.0 %all-gather.8.cloned.1.call-start = ((), (), s32[]{:S(2)}) async-start(), calls=%async_computation.3 | async-start | bytes 4128768 | tf_op jit(solution)/shard_map/all_gather | solution.py:32
  9.4 73.9 %copy-start.2 = (bf16[384,1792]{1,0:T(8,128)(2,1)S(1)}, bf16[384,1792]{1,0:T(8,128)(2,1)}, u32[]{:S(2)}) copy-start(bf16[384,1792]{1,0:T(8,128)(2,1)} %param.10) | copy-start | bytes 4128772
  9.4 194.9 %all-gather.14.cloned.1.call-start = ((), (), s32[]{:S(2)}) async-start(), calls=%async_computation.6 | async-start | bytes 7077888 | tf_op jit(solution)/shard_map/all_gather | solution.py:56
  126.0 0.9 copy-start.7
  126.0 148.4 %all-gather.12.cloned.1.call-start = ((), (), s32[]{:S(2)}) async-start(), calls=%async_computation.5 | async-start | bytes 14155776 | tf_op jit(solution)/shard_map/all_gather | solution.py:55
  128.2 1.3 copy-start.1
  131.1 29.4 %all-to-all-start.1 = ((bf16[384,8,224]{0,2,1:T(8,128)(2,1)}), bf16[384,8,224]{0,2,1:T(8,128)(2,1)S(1)}, u32[]{:S(2)}, u32[]{:S(2)}) async-start(bf16[384,8,224]{0,2,1:T(8,128)(2,1)} %bitcast.3), calls=%async_computation.1 | async-start | bytes 2752512 | tf_op jit(solution)/shard_map/all_to_all | solution.py:53
  160.5 37.1 %all-to-all-start = ((bf16[384,8,224]{0,2,1:T(8,128)(2,1)}), bf16[384,8,224]{0,2,1:T(8,128)(2,1)S(1)}, u32[]{:S(2)}, u32[]{:S(2)}) async-start(bf16[384,8,224]{0,2,1:T(8,128)(2,1)} %bitcast), calls=%async_computation | async-start | bytes 2752512 | tf_op jit(solution)/shard_map/all_to_all | solution.py:52
  164.1 335.3 %all-reduce.2.cloned.1.call-start = ((), (), s32[]{:S(2)}) async-start(), calls=%async_computation.7 | async-start | bytes 786432 | tf_op jit(solution)/shard_map/psum | solution.py:72
  197.6 1.3 copy-start.8
  198.9 5.4 %copy-start.4 = (bf16[8,28,8,384]{3,2,0,1:T(8,128)(2,1)S(1)}, bf16[8,28,8,384]{3,2,0,1:T(8,128)(2,1)}, u32[]{:S(2)}) copy-start(bf16[8,28,8,384]{3,2,0,1:T(8,128)(2,1)} %copy.25) | copy-start | bytes 4128772
  204.3 70.1 %copy-start.5 = (bf16[8,28,8,384]{3,2,0,1:T(8,128)(2,1)S(1)}, bf16[8,28,8,384]{3,2,0,1:T(8,128)(2,1)}, u32[]{:S(2)}) copy-start(bf16[8,28,8,384]{3,2,0,1:T(8,128)(2,1)} %copy.24) | copy-start | bytes 4128772
  274.4 6.4 %copy-start.3 = (bf16[1,224,3072]{2,1,0:T(8,128)(2,1)S(1)}, bf16[1,224,3072]{2,1,0:T(8,128)(2,1)}, u32[]{:S(2)}) copy-start(bf16[1,224,3072]{2,1,0:T(8,128)(2,1)} %param.15) | copy-start | bytes 4128772
  274.4 6.4 %copy-start.6 = (f32[224,1024]{1,0:T(8,128)S(1)}, f32[224,1024]{1,0:T(8,128)}, u32[]{:S(2)}) copy-start(f32[224,1024]{1,0:T(8,128)} %convolution_bitcast_fusion.1) | copy-start | bytes 2752516
  280.8 1.0 copy-start.16
  369.2 3.1 copy-start.9
  370.2 2.8 copy-start.14
  373.8 5.7 %copy-start.10 = (f32[32,224]{1,0:T(8,128)S(1)}, f32[32,224]{1,0:T(8,128)}, u32[]{:S(2)}) copy-start(f32[32,224]{1,0:T(8,128)} %fusion.32) | copy-start | bytes 86020
  373.8 5.7 %copy-start.12 = (f32[32,224]{1,0:T(8,128)S(1)}, f32[32,224]{1,0:T(8,128)}, u32[]{:S(2)}) copy-start(f32[32,224]{1,0:T(8,128)} %fusion.31) | copy-start | bytes 86020
  373.8 5.7 %copy-start.15 = (f32[32,224]{1,0:T(8,128)S(1)}, f32[32,224]{1,0:T(8,128)}, u32[]{:S(2)}) copy-start(f32[32,224]{1,0:T(8,128)} %copy-done.14) | copy-start | bytes 86020
  379.5 122.7 %copy-start.13 = (f32[32,224]{1,0:T(8,128)S(1)}, f32[32,224]{1,0:T(8,128)}, u32[]{:S(2)}) copy-start(f32[32,224]{1,0:T(8,128)} %fusion.31) | copy-start | bytes 86020
  500.4 3.7 copy-start
  500.4 2.7 copy-start.11
Sparse Core Ops, SparseCore 0:
  9.9 37.0 all-gather.5
  48.9 34.3 all-gather.9
  85.2 34.3 all-gather.7
  126.1 74.4 all-gather.13
  202.4 71.9 all-gather.11
  373.9 125.4 all-reduce.1
where the time goes:
time: 514 us; the launch traced here: 512 us
  waiting for transfers between devices  342 us (67%)
  matrix products  54.2 us (11%)
  blocking collectives  44.5 us (9%)
  other arithmetic  35.7 us (7%)
  between operations  14.4 us (3%)
  local copies, waits for them, and re-layouts  13.4 us (3%)
  starting transfers between devices  7.6 us (1%)
    psum x1, waiting for transfers between devices, on_device(): q_new = lax.psum(col_terms, ('node', 'grp')) / group_count  119 us
    all_gather x1, waiting for transfers between devices, on_device(): piece_gu = lax.all_gather(gate_up, 'node', axis=0, tiled=True)  64.7 us
    all_gather x1, waiting for transfers between devices, on_device(): lax.all_gather(down_weight_t, 'node', axis=0, tiled=True)  37.6 us
    all_to_all x1, waiting for transfers between devices, on_device(): lax.all_to_all(tokens, 'node', split_axis=1, concat_axis=0, tiled=True)  31.9 us
    all_gather x1, waiting for transfers between devices, on_device(): lax.all_gather(up_weight, 'node', axis=0, tiled=True)  31.5 us
    all_gather x1, waiting for transfers between devices, on_device(): lax.all_gather(gate_weight, 'node', axis=0, tiled=True)  31.1 us
    all_to_all x1, waiting for transfers between devices, on_device(): lax.all_to_all(cotangent, 'node', split_axis=1, concat_axis=0, tiled=True)  24.3 us
    psum x1, blocking collectives, on_device(): gram_matrix = lax.psum(local_gram, 'node')  24 us
  transfers between devices with their start and end apart: 8, of which 7 were waited for; matrix products, arithmetic and copies ran while one was open for 7% of the time, Pallas kernels for 0%

commit v1 on v0

--- a/solution.py
+++ b/solution.py
@@ -50,7 +50,12 @@
     gate_up = jnp.concatenate([grad_gate, grad_up], axis=1)
     token_cols, cot_cols = (
         lax.all_to_all(tokens, "node", split_axis=1, concat_axis=0, tiled=True),
-        lax.all_to_all(cotangent, "node", split_axis=1, concat_axis=0, tiled=True),
+        jnp.concatenate(
+            lax.all_to_all(
+                jnp.stack(jnp.split(cotangent, lax.axis_size("node"), axis=1)), "node", 0, 0
+            ),
+            axis=0,
+        ),
     )
     piece_gu = lax.all_gather(gate_up, "node", axis=0, tiled=True)
     piece_hidden = lax.all_gather(hidden, "node", axis=0, tiled=True)

time: 514 us -> 478 us (0.930)
  waiting for transfers between devices: 342 us -> 313 us
  other arithmetic: 35.7 us -> 30.5 us
  local copies, waits for them, and re-layouts: 13.4 us -> 18.6 us
    all_gather x1, waiting for transfers between devices: 64.7 us -> 46.4 us  [on_device(): piece_gu = lax.all_gather(gate_up, 'node', axis=0, tiled=True)]
    all_to_all x1, waiting for transfers between devices: 31.9 us -> 18.4 us  [on_device(): lax.all_to_all(tokens, 'node', split_axis=1, concat_axis=0, tiled=True)]
    unnamed x36 -> x56, local copies, waits for them, and re-layouts: 5.8 us -> 13.7 us
    all_gather x1, waiting for transfers between devices: 37.6 us -> 31.1 us  [on_device(): lax.all_gather(down_weight_t, 'node', axis=0, tiled=True)]
    all_gather x1, waiting for transfers between devices: 31.1 us -> 37.6 us  [on_device(): lax.all_gather(gate_weight, 'node', axis=0, tiled=True)]
  transfers between devices with their start and end apart: 8 -> 8, of which waited for: 7 -> 7; matrix products, arithmetic and copies ran while one was open for 7% -> 10% of each run, Pallas kernels for 0% -> 0%
where the time goes in v1:
time: 478 us; the launch traced here: 477 us
  waiting for transfers between devices  313 us (65%)
  matrix products  50.7 us (11%)
  blocking collectives  42.3 us (9%)
  other arithmetic  30.5 us (6%)
  local copies, waits for them, and re-layouts  18.6 us (4%)
  between operations  14.5 us (3%)
  starting transfers between devices  7.56 us (2%)
    psum x1, waiting for transfers between devices, on_device(): q_new = lax.psum(col_terms, ('node', 'grp')) / group_count  119 us
    all_gather x1, waiting for transfers between devices, on_device(): piece_gu = lax.all_gather(gate_up, 'node', axis=0, tiled=True)  46.4 us
    all_gather x1, waiting for transfers between devices, on_device(): lax.all_gather(gate_weight, 'node', axis=0, tiled=True)  37.6 us
    all_gather x1, waiting for transfers between devices, on_device(): lax.all_gather(up_weight, 'node', axis=0, tiled=True)  31.5 us
    all_gather x1, waiting for transfers between devices, on_device(): lax.all_gather(down_weight_t, 'node', axis=0, tiled=True)  31.1 us
    all_to_all x1, waiting for transfers between devices, on_device(): lax.all_to_all(jnp.stack(jnp.split(cotangent, lax.axis_size('node'), axis...  27 us
    psum x1, blocking collectives, on_device(): gram_matrix = lax.psum(local_gram, 'node')  22.9 us
    psum x1, blocking collectives, on_device(): lax.psum(row_terms.astype(jnp.bfloat16), 'grp').astype(jnp.float32)  19.4 us
  transfers between devices with their start and end apart: 8, of which 7 were waited for; matrix products, arithmetic and copies ran while one was open for 10% of the time, Pallas kernels for 0%

profile of v1, /device:TPU:0, one launch (start us, length us, event | category | flops | bytes accessed | tf_op | source)
XLA Modules:
  0.0 477.5 jit_solution(9719977951039818772)
XLA Ops:
  7.9 0.7 all-gather.6.cloned.1.call-update
  9.4 37.6 %all-gather.10.cloned.1.call-done = bf16[1792,1024]{1,0:T(8,128)(2,1)} async-done(((bf16[224,1024]{1,0:T(8,128)(2,1)}), bf16[1792,1024]{1,0:T(8,128)(2,1)}) %all-gather.10.cloned.1.call-update) | async-done | bytes 3670032 | tf_op jit(solution)/shard_map/all_gather | solution.py:31
  47.0 5.2 %fusion.46 = f32[384,1024]{1,0:T(8,128)} fusion(bf16[384,1792]{1,0:T(8,128)(2,1)} %param.10, bf16[1792,1024]{1,0:T(8,128)(2,1)} %all-gather.10.cloned.1.call-done), kind=kOutput, calls=%fused_computation.101 | convolution fusion | flops 1409286144 | bytes 6619136 | tf_op jit(solution)/shard_map/dot_general | solution.py:35
  52.2 31.1 %all-gather.6.cloned.1.call-done = bf16[1792,1024]{1,0:T(8,128)(2,1)} async-done(((bf16[224,1024]{1,0:T(8,128)(2,1)}), bf16[1792,1024]{1,0:T(8,128)(2,1)}) %all-gather.6.cloned.1.call-update) | async-done | bytes 3670032 | tf_op jit(solution)/shard_map/all_gather | solution.py:33
  83.3 4.8 %fusion.45 = f32[384,1024]{1,0:T(8,128)} fusion(bf16[384,1792]{1,0:T(8,128)(2,1)S(1)} %copy-done, bf16[1792,1024]{1,0:T(8,128)(2,1)} %all-gather.6.cloned.1.call-done), kind=kOutput, calls=%fused_computation.100 | convolution fusion | flops 1409286144 | bytes 6619136 | tf_op jit(solution)/shard_map/dot_general | solution.py:39
  88.1 31.5 %all-gather.8.cloned.1.call-done = bf16[1792,1024]{1,0:T(8,128)(2,1)} async-done(((bf16[224,1024]{1,0:T(8,128)(2,1)}), bf16[1792,1024]{1,0:T(8,128)(2,1)}) %all-gather.8.cloned.1.call-update) | async-done | bytes 3670032 | tf_op jit(solution)/shard_map/all_gather | solution.py:32
  119.6 6.7 %multiply_convert_fusion = (bf16[384,1024]{1,0:T(8,128)(2,1)}, bf16[384,1024]{1,0:T(8,128)(2,1)}, bf16[384,1024]{1,0:T(8,128)(2,1)S(1)}) fusion(f32[384,1024]{1,0:T(8,128)} %fusion.46, f32[384,1024]{1,0:T(8,128)} %fusion.45, bf16[384,1792]{1,0:T(8,128)(2,1)S(1)} %copy-done.2, bf16[1792,1024]{1,0:T(8,128)(2,1)} %all-gather.8.cloned.1.call-done), kind=kOutput, calls=%fused_computation.15 | convolution fusion | flops 1419116544 | bytes 10551296 | tf_op jit(solution)/shard_map/dot_general | solution.py:36
  126.4 2.7 pad_maximum_fusion
  129.1 1.3 fusion.44
  130.5 1.1 copy.51
  131.5 1.1 copy.52
  132.6 1.1 copy.53
  133.7 1.1 copy.54
  135.5 0.7 bitcast_dynamic-update-slice_fusion.7
  141.0 3.6 all-to-all-start.1
  144.6 1.5 copy.35
  146.1 27.0 %all-to-all-done.1 = bf16[8,384,224]{1,2,0:T(8,128)(2,1)S(1)} async-done(((bf16[8,384,224]{1,2,0:T(8,128)(2,1)}), bf16[8,384,224]{1,2,0:T(8,128)(2,1)S(1)}, u32[]{:S(2)}, u32[]{:S(2)}) %all-to-all-start.1) | async-done | bytes 1376288 | tf_op jit(solution)/shard_map/all_to_all | solution.py:54
  173.1 3.6 all-to-all-start
  177.0 1.3 copy.60
  178.3 18.4 %all-to-all-done = bf16[384,8,224]{0,2,1:T(8,128)(2,1)S(1)} async-done(((bf16[384,8,224]{0,2,1:T(8,128)(2,1)}), bf16[384,8,224]{0,2,1:T(8,128)(2,1)S(1)}, u32[]{:S(2)}, u32[]{:S(2)}) %all-to-all-start) | async-done | bytes 1376288 | tf_op jit(solution)/shard_map/all_to_all | solution.py:52
  196.7 1.3 copy.59
  198.0 5.3 %fusion.47 = f32[384,1792]{1,0:T(8,128)} fusion(bf16[384,1024]{1,0:T(8,128)(2,1)S(1)} %copy-done.9, bf16[1792,1024]{1,0:T(8,128)(2,1)} %all-gather.10.cloned.1.call-done), kind=kOutput, calls=%fused_computation.102 | convolution fusion | flops 1409286144 | bytes 7208960 | tf_op jit(solution)/shard_map/dot_general | solution.py:43
  203.3 5.4 %fusion.48 = f32[224,1024]{1,0:T(8,128)} fusion(bf16[3072,224]{0,1:T(8,128)(2,1)S(1)} %bitcast.145, bf16[3072,1024]{1,0:T(8,128)(2,1)} %all-gather.14.cloned.1.call-done), kind=kOutput, calls=%fused_computation.103 | convolution fusion | flops 1409286144 | bytes 8585216 | tf_op jit(solution)/shard_map/dot_general | solution.py:20
  208.7 46.4 %all-gather.12.cloned.1.call-done = bf16[3072,2048]{1,0:T(8,128)(2,1)} async-done(((bf16[384,2048]{1,0:T(8,128)(2,1)}), bf16[3072,2048]{1,0:T(8,128)(2,1)}) %all-gather.12.cloned.1.call-update) | async-done | bytes 12582928 | tf_op jit(solution)/shard_map/all_gather | solution.py:60
  255.1 6.4 %convolution_bitcast_fusion = f32[224,2048]{1,0:T(8,128)S(1)} fusion(bf16[3072,224]{0,1:T(8,128)(2,1)S(1)} %bitcast.146, bf16[3072,2048]{1,0:T(8,128)(2,1)} %all-gather.12.cloned.1.call-done), kind=kOutput, calls=%fused_computation.4 | convolution fusion | flops 2818572288 | bytes 15794176 | tf_op jit(solution)/shard_map/dot_general | solution.py:20
  262.5 0.9 fusion.17
  263.4 0.9 fusion.16
  264.3 0.9 fusion.15
  265.2 19.4 %psum.21 = bf16[3,224,32]{1,2,0:T(8,128)(2,1)S(1)} all-reduce(bf16[3,224,32]{1,2,0:T(8,128)(2,1)S(1)} %pad_maximum_fusion.4), channel_id=1, replica_groups=mesh['node'=8,'grp'=4] {'grp'}, use_global_device_ids=true, to_apply=%region_0.0 | all-reduce | flops 21504 | bytes 86016 | tf_op jit(solution)/shard_map/psum | solution.py:69
  284.9 22.9 %psum.22 = f32[3,32,32]{1,2,0:T(8,128)S(1)} all-reduce(f32[3,32,32]{1,2,0:T(8,128)S(1)} %fusion.33), channel_id=1, replica_groups=mesh['node'=8,'grp'=4] {'node'}, use_global_device_ids=true, to_apply=%region_1.0 | all-reduce | flops 3072 | bytes 24576 | tf_op jit(solution)/shard_map/psum | solution.py:71
  308.7 2.9 cholesky.81
  312.9 2.4 custom-call.9
  316.2 1.3 convolution_bitcast_fusion.1
  317.6 2.9 cholesky.70
  321.8 2.4 custom-call.8
  325.1 1.3 convolution_bitcast_fusion.2
  326.4 3.6 cholesky.59
  330.8 1.2 fusion.34
  332.0 3.2 custom-call.7
  335.2 1.0 fusion.32
  337.4 1.7 pad_maximum_fusion.2
  339.2 5.7 %fusion = bf16[384,1792]{1,0:T(8,128)(2,1)} fusion(f32[384,1792]{1,0:T(8,128)} %fusion.47, bf16[384,1024]{1,0:T(8,128)(2,1)S(1)} %copy-done.8, bf16[1792,1024]{1,0:T(8,128)(2,1)} %all-gather.8.cloned.1.call-done), kind=kOutput, calls=%fused_computation.1 | convolution fusion | flops 1410662400 | bytes 8585216 | tf_op jit(solution)/shard_map/dot_general | solution.py:46
  345.6 119.2 %all-reduce.2.cloned.1.call-done = f32[3,1024,32]{1,2,0:T(8,128)} async-done(((f32[3,1024,32]{1,2,0:T(8,128)}), f32[3,1024,32]{1,2,0:T(8,128)}) %all-reduce.2.cloned.1.call-update) | async-done | bytes 393232 | tf_op jit(solution)/shard_map/psum | solution.py:77
  464.8 1.0 broadcast_multiply_fusion
  465.8 1.8 fusion.12
  467.6 0.9 fusion.13
  468.5 0.9 fusion.14
  469.5 1.2 pad_maximum_fusion.1
  (84 shorter events, 16.3 us)
Async XLA Ops:
  7.2 39.8 %all-gather.10.cloned.1.call-start = ((), (), s32[]{:S(2)}) async-start(), calls=%async_computation.4 | async-start | bytes 4128768 | tf_op jit(solution)/shard_map/all_gather | solution.py:31
  7.9 75.4 %all-gather.6.cloned.1.call-start = ((), (), s32[]{:S(2)}) async-start(), calls=%async_computation.2 | async-start | bytes 4128768 | tf_op jit(solution)/shard_map/all_gather | solution.py:33
  8.6 111.0 %all-gather.8.cloned.1.call-start = ((), (), s32[]{:S(2)}) async-start(), calls=%async_computation.3 | async-start | bytes 4128768 | tf_op jit(solution)/shard_map/all_gather | solution.py:32
  9.4 73.9 %copy-start = (bf16[384,1792]{1,0:T(8,128)(2,1)S(1)}, bf16[384,1792]{1,0:T(8,128)(2,1)}, u32[]{:S(2)}) copy-start(bf16[384,1792]{1,0:T(8,128)(2,1)} %param.11) | copy-start | bytes 4128772
  9.4 193.9 %all-gather.14.cloned.1.call-start = ((), (), s32[]{:S(2)}) async-start(), calls=%async_computation.6 | async-start | bytes 7077888 | tf_op jit(solution)/shard_map/all_gather | solution.py:61
  52.2 67.4 %copy-start.2 = (bf16[384,1792]{1,0:T(8,128)(2,1)S(1)}, bf16[384,1792]{1,0:T(8,128)(2,1)}, u32[]{:S(2)}) copy-start(bf16[384,1792]{1,0:T(8,128)(2,1)} %param.10) | copy-start | bytes 4128772
  126.3 2.8 copy-start.7
  126.3 128.8 %all-gather.12.cloned.1.call-start = ((), (), s32[]{:S(2)}) async-start(), calls=%async_computation.5 | async-start | bytes 14155776 | tf_op jit(solution)/shard_map/all_gather | solution.py:60
  141.0 32.2 %all-to-all-start.1 = ((bf16[8,384,224]{1,2,0:T(8,128)(2,1)}), bf16[8,384,224]{1,2,0:T(8,128)(2,1)S(1)}, u32[]{:S(2)}, u32[]{:S(2)}) async-start(bf16[8,384,224]{1,2,0:T(8,128)(2,1)} %bitcast_dynamic-update-slice_fusion), calls=%async_computation.1 | async-start | bytes 2752512 | tf_op jit(solution)/shard_map/all_to_all | solution.py:54
  173.1 23.6 %all-to-all-start = ((bf16[384,8,224]{0,2,1:T(8,128)(2,1)}), bf16[384,8,224]{0,2,1:T(8,128)(2,1)S(1)}, u32[]{:S(2)}, u32[]{:S(2)}) async-start(bf16[384,8,224]{0,2,1:T(8,128)(2,1)} %bitcast), calls=%async_computation | async-start | bytes 2752512 | tf_op jit(solution)/shard_map/all_to_all | solution.py:52
  176.7 288.0 %all-reduce.2.cloned.1.call-start = ((), (), s32[]{:S(2)}) async-start(), calls=%async_computation.7 | async-start | bytes 786432 | tf_op jit(solution)/shard_map/psum | solution.py:77
  178.3 19.8 %copy-start.9 = (bf16[384,1024]{1,0:T(8,128)(2,1)S(1)}, bf16[384,1024]{1,0:T(8,128)(2,1)}, u32[]{:S(2)}) copy-start(bf16[384,1024]{1,0:T(8,128)(2,1)} %get-tuple-element.7) | copy-start | bytes 2359300
  198.0 5.3 %copy-start.4 = (bf16[8,28,8,384]{3,2,0,1:T(8,128)(2,1)S(1)}, bf16[8,28,8,384]{3,2,0,1:T(8,128)(2,1)}, u32[]{:S(2)}) copy-start(bf16[8,28,8,384]{3,2,0,1:T(8,128)(2,1)} %copy.60) | copy-start | bytes 4128772
  203.3 51.8 %copy-start.5 = (bf16[8,28,8,384]{3,2,0,1:T(8,128)(2,1)S(1)}, bf16[8,28,8,384]{3,2,0,1:T(8,128)(2,1)}, u32[]{:S(2)}) copy-start(bf16[8,28,8,384]{3,2,0,1:T(8,128)(2,1)} %copy.59) | copy-start | bytes 4128772
  255.1 6.4 %copy-start.3 = (bf16[1,224,3072]{2,1,0:T(8,128)(2,1)S(1)}, bf16[1,224,3072]{2,1,0:T(8,128)(2,1)}, u32[]{:S(2)}) copy-start(bf16[1,224,3072]{2,1,0:T(8,128)(2,1)} %param.15) | copy-start | bytes 4128772
  255.1 6.4 %copy-start.6 = (f32[224,1024]{1,0:T(8,128)S(1)}, f32[224,1024]{1,0:T(8,128)}, u32[]{:S(2)}) copy-start(f32[224,1024]{1,0:T(8,128)} %fusion.48) | copy-start | bytes 2752516
  261.5 1.0 copy-start.19
  284.6 39.6 %copy-start.18 = (f32[3,224,32]{1,2,0:T(8,128)}, f32[3,224,32]{1,2,0:T(8,128)S(1)}, u32[]{:S(2)}) copy-start(f32[3,224,32]{1,2,0:T(8,128)S(1)} %convert_multiply_fusion) | copy-start | bytes 258052
  315.6 0.6 copy-start.10
  324.5 0.6 copy-start.12
  325.1 14.1 %copy-start.8 = (bf16[384,1024]{1,0:T(8,128)(2,1)S(1)}, bf16[384,1024]{1,0:T(8,128)(2,1)}, u32[]{:S(2)}) copy-start(bf16[384,1024]{1,0:T(8,128)(2,1)} %copy-done.7) | copy-start | bytes 2359300
  336.2 0.6 copy-start.15
  339.2 5.7 %copy-start.11 = (f32[32,224]{1,0:T(8,128)S(1)}, f32[32,224]{1,0:T(8,128)}, u32[]{:S(2)}) copy-start(f32[32,224]{1,0:T(8,128)} %copy-done.10) | copy-start | bytes 86020
  339.2 5.7 %copy-start.13 = (f32[32,224]{1,0:T(8,128)S(1)}, f32[32,224]{1,0:T(8,128)}, u32[]{:S(2)}) copy-start(f32[32,224]{1,0:T(8,128)} %copy-done.12) | copy-start | bytes 86020
  339.2 5.7 %copy-start.16 = (f32[32,224]{1,0:T(8,128)S(1)}, f32[32,224]{1,0:T(8,128)}, u32[]{:S(2)}) copy-start(f32[32,224]{1,0:T(8,128)} %copy-done.15) | copy-start | bytes 86020
  344.9 122.7 %copy-start.14 = (f32[32,224]{1,0:T(8,128)S(1)}, f32[32,224]{1,0:T(8,128)}, u32[]{:S(2)}) copy-start(f32[32,224]{1,0:T(8,128)} %copy-done.12) | copy-start | bytes 86020
  465.8 3.7 copy-start.1
  465.8 2.7 copy-start.17
Sparse Core Ops, SparseCore 0:
  9.9 37.0 all-gather.9
  48.9 34.3 all-gather.5
  85.2 34.3 all-gather.7
  126.5 54.5 all-gather.13
  182.8 72.2 all-gather.11
  339.3 125.3 all-reduce.1
